TPU v7x, 512 devices: a 8x2x16 block of a 8x16x16 slice. The times are simulated.
512 devices in a mesh: parts: 2 (over y), blk: 16 (over z), sub: 8 (over x), rep: 2 (over core).
Axes of the slice: x: 8, y: 2, z: 16, core: 2. Of those that a mesh axis runs over, the one named last changes fastest.
The devices are a block of a 8x16x16 slice.
Arguments:
- queries: bfloat16 [2048, 32, 128], P(('parts', 'blk', 'sub', 'rep')), parts along dimension 0, may hold values from -1.5 to 1.5
- passages: bfloat16 [2048, 128, 128], P(('parts', 'blk')), parts along dimension 0, may hold values from -1.5 to 1.5
- lengths: int32 [2048], P(('parts', 'blk')), parts along dimension 0, may hold values from 8 to 128
- slot_of: int32 [2048], P('parts'), parts along dimension 0, may hold values from 0 to 1023, each once
- candidates: int32 [2048, 256], P(('parts', 'blk', 'sub', 'rep')), parts along dimension 0, may hold values from 0 to 1023
Outputs:
- score: float32 [2048, 256], P(('parts', 'blk', 'sub', 'rep')), parts along dimension 0
- top: float32 [2048, 10], P(('parts', 'blk', 'sub', 'rep')), parts along dimension 0
There are 2 independent parts, one for each index of `parts`. A program takes and returns all parts, laid end to end along the dimension named above; each array names one. Nothing has to cross between parts.
Inputs may be any that keep to these rules, and one draw needn't show every extreme that they name: `slot_of`: a permutation; storage row r lies on the blk index r // 64. `candidates`: passage ids, repeats allowed. `lengths`: the live slots of a row are its first ones.
All inputs are finite; a program needn't handle non-finite values.
Results may differ from a plain program's by a relative error of at most 0.0003.
Values may be sent and summed in bfloat16 or wider, within the bound.
A program may use at most 64 MiB of HBM per device.

v0:
```python
import jax
import jax.numpy as jnp
from jax import lax
from jax.sharding import PartitionSpec as P

TOPN = 10


def score_table(rows_q, passages, lengths):
    queries_here = rows_q.shape[0]
    tokens = rows_q.shape[1]
    width = rows_q.shape[2]
    count = passages.shape[0]
    span = passages.shape[1]
    group = 4
    flat = rows_q.reshape(queries_here * tokens, width)
    blocks = passages.reshape(count // group, group * span, width)
    spans = lengths.reshape(count // group, group)

    def one_block(pair):
        piece, live_count = pair
        similar = lax.dot_general(
            flat, piece, (((1,), (1,)), ((), ())), preferred_element_type=jnp.float32
        )
        similar = similar.reshape(queries_here * tokens, group, span)
        live = lax.broadcasted_iota(jnp.int32, (group, span), 1) < live_count[:, None]
        best = jnp.max(jnp.where(live[None], similar, -1e30), axis=2)
        return jnp.sum(best.reshape(queries_here, tokens, group), axis=1) / tokens

    table = lax.map(one_block, (blocks, spans))
    return jnp.transpose(table, (1, 0, 2)).reshape(queries_here, count)


def shards(queries, passages, lengths, slot_of, candidates):
    table = score_table(lax.all_gather(queries, "blk", axis=0, tiled=True), passages, lengths)
    whole = lax.all_to_all(table, "blk", split_axis=0, concat_axis=1, tiled=True)
    score = jnp.take_along_axis(whole, jnp.take(slot_of, candidates, axis=0), axis=1)
    top = lax.top_k(score, TOPN)[0]
    return (score, top)


def solution(mesh):
    return jax.shard_map(
        shards,
        mesh=mesh,
        in_specs=(
            P(("parts", "blk", "sub", "rep"), None, None),
            P(("parts", "blk"), None, None),
            P(("parts", "blk")),
            P("parts"),
            P(("parts", "blk", "sub", "rep"), None),
        ),
        out_specs=(
            P(("parts", "blk", "sub", "rep"), None),
            P(("parts", "blk", "sub", "rep"), None),
        ),
        check_vma=False,
    )
```

profile of v0, /device:TPU:86, one launch (start us, length us, event | category | flops | bytes accessed | tf_op | source)
XLA Modules:
  0.0 134.1 jit_solution(3773919563160055687)
XLA Ops:
  0.7 0.7 reshape.67
  1.4 71.3 %all_gather.3 = bf16[64,32,128]{2,1,0:T(8,128)(2,1)S(1)} all-gather(bf16[4,32,128]{2,1,0:T(8,128)(2,1)} %param.7), channel_id=1, replica_groups=mesh['parts'=2,'blk'=16,'sub'=8,'rep'=2] {'blk'}, dimensions={0}, use_global_device_ids=true | all-gather | bytes 557056 | tf_op jit(solution)/shard_map/all_gather | solution.py:35
  72.6 31.7 %while.10 = (s32[]{:T(128)}, f32[16,64,4]{1,2,0:T(4,128)S(1)}, s32[16,4]{1,0:T(8,128)S(1)}, bf16[16,512,128]{2,1,0:T(8,128)(2,1)}, bf16[2048,128]{1,0:T(8,128)(2,1)S(1)}, /*index=5*/s32[]{:T(128)}, f32[]{:T(128)}) while((s32[]{:T(128)}, f32[16,64,4]{1,2,0:T(4,128)S(1)}, s32[16,4]{1,0:T(8,128)S(1)}, bf16[16,512,128]{2,1,0:T(8,128)(2,1)}, ...), condition=%wide.region_3.4_spmd, body=%wide.region_0.3_spmd.sunk | while | flops 270533120 | bytes 792725 | solution.py:30
  72.7 1.7 %select_reduce_fusion.2 = f32[2048,4]{0,1:T(4,128)S(1)} fusion(pred[4,128]{1,0:T(4,128)(4,1)S(1)} %iota_compare_fusion.2, bf16[2048,128]{1,0:T(8,128)(2,1)S(1)} %get-tuple-element.93, bf16[16,512,128]{2,1,0:T(8,128)(2,1)} %get-tuple-element.92, s32[]{:T(128)S(6)} %copy.19), kind=kOutput, calls=%fused_computation.2.clone.1 | convolution fusion | flops 270524416 | bytes 688644 | tf_op jit(solution)/shard_map/while/body/eval_jaxpr/dot_general | solution.py:22
  74.7 1.6 %select_reduce_fusion.2 = f32[2048,4]{0,1:T(4,128)S(1)} fusion(pred[4,128]{1,0:T(4,128)(4,1)S(1)} %iota_compare_fusion.2, bf16[2048,128]{1,0:T(8,128)(2,1)S(1)} %get-tuple-element.93, bf16[16,512,128]{2,1,0:T(8,128)(2,1)} %get-tuple-element.92, s32[]{:T(128)S(6)} %copy.19), kind=kOutput, calls=%fused_computation.2.clone.1 | convolution fusion | flops 270524416 | bytes 688644 | tf_op jit(solution)/shard_map/while/body/eval_jaxpr/dot_general | solution.py:22
  76.7 1.6 %select_reduce_fusion.2 = f32[2048,4]{0,1:T(4,128)S(1)} fusion(pred[4,128]{1,0:T(4,128)(4,1)S(1)} %iota_compare_fusion.2, bf16[2048,128]{1,0:T(8,128)(2,1)S(1)} %get-tuple-element.93, bf16[16,512,128]{2,1,0:T(8,128)(2,1)} %get-tuple-element.92, s32[]{:T(128)S(6)} %copy.19), kind=kOutput, calls=%fused_computation.2.clone.1 | convolution fusion | flops 270524416 | bytes 688644 | tf_op jit(solution)/shard_map/while/body/eval_jaxpr/dot_general | solution.py:22
  78.7 1.6 %select_reduce_fusion.2 = f32[2048,4]{0,1:T(4,128)S(1)} fusion(pred[4,128]{1,0:T(4,128)(4,1)S(1)} %iota_compare_fusion.2, bf16[2048,128]{1,0:T(8,128)(2,1)S(1)} %get-tuple-element.93, bf16[16,512,128]{2,1,0:T(8,128)(2,1)} %get-tuple-element.92, s32[]{:T(128)S(6)} %copy.19), kind=kOutput, calls=%fused_computation.2.clone.1 | convolution fusion | flops 270524416 | bytes 688644 | tf_op jit(solution)/shard_map/while/body/eval_jaxpr/dot_general | solution.py:22
  80.7 1.6 %select_reduce_fusion.2 = f32[2048,4]{0,1:T(4,128)S(1)} fusion(pred[4,128]{1,0:T(4,128)(4,1)S(1)} %iota_compare_fusion.2, bf16[2048,128]{1,0:T(8,128)(2,1)S(1)} %get-tuple-element.93, bf16[16,512,128]{2,1,0:T(8,128)(2,1)} %get-tuple-element.92, s32[]{:T(128)S(6)} %copy.19), kind=kOutput, calls=%fused_computation.2.clone.1 | convolution fusion | flops 270524416 | bytes 688644 | tf_op jit(solution)/shard_map/while/body/eval_jaxpr/dot_general | solution.py:22
  82.6 1.6 %select_reduce_fusion.2 = f32[2048,4]{0,1:T(4,128)S(1)} fusion(pred[4,128]{1,0:T(4,128)(4,1)S(1)} %iota_compare_fusion.2, bf16[2048,128]{1,0:T(8,128)(2,1)S(1)} %get-tuple-element.93, bf16[16,512,128]{2,1,0:T(8,128)(2,1)} %get-tuple-element.92, s32[]{:T(128)S(6)} %copy.19), kind=kOutput, calls=%fused_computation.2.clone.1 | convolution fusion | flops 270524416 | bytes 688644 | tf_op jit(solution)/shard_map/while/body/eval_jaxpr/dot_general | solution.py:22
  84.6 1.6 %select_reduce_fusion.2 = f32[2048,4]{0,1:T(4,128)S(1)} fusion(pred[4,128]{1,0:T(4,128)(4,1)S(1)} %iota_compare_fusion.2, bf16[2048,128]{1,0:T(8,128)(2,1)S(1)} %get-tuple-element.93, bf16[16,512,128]{2,1,0:T(8,128)(2,1)} %get-tuple-element.92, s32[]{:T(128)S(6)} %copy.19), kind=kOutput, calls=%fused_computation.2.clone.1 | convolution fusion | flops 270524416 | bytes 688644 | tf_op jit(solution)/shard_map/while/body/eval_jaxpr/dot_general | solution.py:22
  86.6 1.6 %select_reduce_fusion.2 = f32[2048,4]{0,1:T(4,128)S(1)} fusion(pred[4,128]{1,0:T(4,128)(4,1)S(1)} %iota_compare_fusion.2, bf16[2048,128]{1,0:T(8,128)(2,1)S(1)} %get-tuple-element.93, bf16[16,512,128]{2,1,0:T(8,128)(2,1)} %get-tuple-element.92, s32[]{:T(128)S(6)} %copy.19), kind=kOutput, calls=%fused_computation.2.clone.1 | convolution fusion | flops 270524416 | bytes 688644 | tf_op jit(solution)/shard_map/while/body/eval_jaxpr/dot_general | solution.py:22
  88.6 1.6 %select_reduce_fusion.2 = f32[2048,4]{0,1:T(4,128)S(1)} fusion(pred[4,128]{1,0:T(4,128)(4,1)S(1)} %iota_compare_fusion.2, bf16[2048,128]{1,0:T(8,128)(2,1)S(1)} %get-tuple-element.93, bf16[16,512,128]{2,1,0:T(8,128)(2,1)} %get-tuple-element.92, s32[]{:T(128)S(6)} %copy.19), kind=kOutput, calls=%fused_computation.2.clone.1 | convolution fusion | flops 270524416 | bytes 688644 | tf_op jit(solution)/shard_map/while/body/eval_jaxpr/dot_general | solution.py:22
  90.6 1.6 %select_reduce_fusion.2 = f32[2048,4]{0,1:T(4,128)S(1)} fusion(pred[4,128]{1,0:T(4,128)(4,1)S(1)} %iota_compare_fusion.2, bf16[2048,128]{1,0:T(8,128)(2,1)S(1)} %get-tuple-element.93, bf16[16,512,128]{2,1,0:T(8,128)(2,1)} %get-tuple-element.92, s32[]{:T(128)S(6)} %copy.19), kind=kOutput, calls=%fused_computation.2.clone.1 | convolution fusion | flops 270524416 | bytes 688644 | tf_op jit(solution)/shard_map/while/body/eval_jaxpr/dot_general | solution.py:22
  92.5 1.6 %select_reduce_fusion.2 = f32[2048,4]{0,1:T(4,128)S(1)} fusion(pred[4,128]{1,0:T(4,128)(4,1)S(1)} %iota_compare_fusion.2, bf16[2048,128]{1,0:T(8,128)(2,1)S(1)} %get-tuple-element.93, bf16[16,512,128]{2,1,0:T(8,128)(2,1)} %get-tuple-element.92, s32[]{:T(128)S(6)} %copy.19), kind=kOutput, calls=%fused_computation.2.clone.1 | convolution fusion | flops 270524416 | bytes 688644 | tf_op jit(solution)/shard_map/while/body/eval_jaxpr/dot_general | solution.py:22
  94.5 1.6 %select_reduce_fusion.2 = f32[2048,4]{0,1:T(4,128)S(1)} fusion(pred[4,128]{1,0:T(4,128)(4,1)S(1)} %iota_compare_fusion.2, bf16[2048,128]{1,0:T(8,128)(2,1)S(1)} %get-tuple-element.93, bf16[16,512,128]{2,1,0:T(8,128)(2,1)} %get-tuple-element.92, s32[]{:T(128)S(6)} %copy.19), kind=kOutput, calls=%fused_computation.2.clone.1 | convolution fusion | flops 270524416 | bytes 688644 | tf_op jit(solution)/shard_map/while/body/eval_jaxpr/dot_general | solution.py:22
  96.5 1.6 %select_reduce_fusion.2 = f32[2048,4]{0,1:T(4,128)S(1)} fusion(pred[4,128]{1,0:T(4,128)(4,1)S(1)} %iota_compare_fusion.2, bf16[2048,128]{1,0:T(8,128)(2,1)S(1)} %get-tuple-element.93, bf16[16,512,128]{2,1,0:T(8,128)(2,1)} %get-tuple-element.92, s32[]{:T(128)S(6)} %copy.19), kind=kOutput, calls=%fused_computation.2.clone.1 | convolution fusion | flops 270524416 | bytes 688644 | tf_op jit(solution)/shard_map/while/body/eval_jaxpr/dot_general | solution.py:22
  98.5 1.6 %select_reduce_fusion.2 = f32[2048,4]{0,1:T(4,128)S(1)} fusion(pred[4,128]{1,0:T(4,128)(4,1)S(1)} %iota_compare_fusion.2, bf16[2048,128]{1,0:T(8,128)(2,1)S(1)} %get-tuple-element.93, bf16[16,512,128]{2,1,0:T(8,128)(2,1)} %get-tuple-element.92, s32[]{:T(128)S(6)} %copy.19), kind=kOutput, calls=%fused_computation.2.clone.1 | convolution fusion | flops 270524416 | bytes 688644 | tf_op jit(solution)/shard_map/while/body/eval_jaxpr/dot_general | solution.py:22
  100.5 1.6 %select_reduce_fusion.2 = f32[2048,4]{0,1:T(4,128)S(1)} fusion(pred[4,128]{1,0:T(4,128)(4,1)S(1)} %iota_compare_fusion.2, bf16[2048,128]{1,0:T(8,128)(2,1)S(1)} %get-tuple-element.93, bf16[16,512,128]{2,1,0:T(8,128)(2,1)} %get-tuple-element.92, s32[]{:T(128)S(6)} %copy.19), kind=kOutput, calls=%fused_computation.2.clone.1 | convolution fusion | flops 270524416 | bytes 688644 | tf_op jit(solution)/shard_map/while/body/eval_jaxpr/dot_general | solution.py:22
  102.4 1.6 %select_reduce_fusion.2 = f32[2048,4]{0,1:T(4,128)S(1)} fusion(pred[4,128]{1,0:T(4,128)(4,1)S(1)} %iota_compare_fusion.2, bf16[2048,128]{1,0:T(8,128)(2,1)S(1)} %get-tuple-element.93, bf16[16,512,128]{2,1,0:T(8,128)(2,1)} %get-tuple-element.92, s32[]{:T(128)S(6)} %copy.19), kind=kOutput, calls=%fused_computation.2.clone.1 | convolution fusion | flops 270524416 | bytes 688644 | tf_op jit(solution)/shard_map/while/body/eval_jaxpr/dot_general | solution.py:22
  105.6 3.9 %all-to-all-start = ((f32[16,1,256]{2,1,0:T(1,128)}), f32[16,1,256]{2,1,0:T(1,128)S(1)}, u32[]{:S(2)}, u32[]{:S(2)}) async-start(f32[16,1,256]{2,1,0:T(1,128)} %reshape.92), calls=%async_computation | async-start | bytes 32768 | tf_op jit(solution)/shard_map/all_to_all | solution.py:36
  109.6 4.5 %gather_fusion = s32[1024]{0:T(1024)S(1)} fusion(s32[1024]{0:T(1024)S(1)} %copy-done, s32[1024]{0:T(1024)S(1)} %broadcast_clamp_fusion), kind=kCustom, calls=%fused_computation | custom fusion | bytes 12288 | tf_op jit(solution)/shard_map/jit(_take)/gather | solution.py:37
  114.2 7.5 %all-to-all-done = f32[16,1,256]{2,1,0:T(1,128)S(1)} async-done(((f32[16,1,256]{2,1,0:T(1,128)}), f32[16,1,256]{2,1,0:T(1,128)S(1)}, u32[]{:S(2)}, u32[]{:S(2)}) %all-to-all-start) | async-done | bytes 16416 | tf_op jit(solution)/shard_map/all_to_all | solution.py:36
  123.0 9.1 %gather_fusion.1 = f32[1024]{0:T(1024)S(1)} fusion(f32[4,1024]{1,0:T(4,128)S(1)} %all_to_all.17, s32[1024]{0:T(1024)S(1)} %bitcast.43), kind=kCustom, calls=%fused_computation.1 | custom fusion | bytes 16384 | tf_op jit(solution)/shard_map/jit(take_along_axis)/gather | solution.py:37
  132.2 1.9 %sort_prefixfusion = f32[4,10]{1,0:T(4,128)} fusion(f32[4,256]{1,0:T(4,128)S(1)} %and_select_fusion), kind=kCustom, calls=%top_k.9.sort_prefix | custom fusion | flops 10240 | bytes 4256 | tf_op jit(solution)/shard_map/top_k | solution.py:38
  (103 shorter events, 7.6 us)
Async XLA Ops:
  0.6 109.0 %copy-start = (s32[1024]{0:T(1024)S(1)}, s32[1024]{0:T(1024)}, u32[]{:S(2)}) copy-start(s32[1024]{0:T(1024)} %param.10) | copy-start | bytes 12292
  72.6 36.9 %copy-start.1 = (s32[4,256]{1,0:T(4,128)S(1)}, s32[4,256]{1,0:T(4,128)}, u32[]{:S(2)}) copy-start(s32[4,256]{1,0:T(4,128)} %param.11) | copy-start | bytes 12292
  105.6 16.0 %all-to-all-start = ((f32[16,1,256]{2,1,0:T(1,128)}), f32[16,1,256]{2,1,0:T(1,128)S(1)}, u32[]{:S(2)}, u32[]{:S(2)}) async-start(f32[16,1,256]{2,1,0:T(1,128)} %reshape.92), calls=%async_computation | async-start | bytes 32768 | tf_op jit(solution)/shard_map/all_to_all | solution.py:36
  132.2 1.9 %copy-start.2 = (f32[4,256]{1,0:T(4,128)}, f32[4,256]{1,0:T(4,128)S(1)}, u32[]{:S(2)}) copy-start(f32[4,256]{1,0:T(4,128)S(1)} %and_select_fusion) | copy-start | bytes 12292
where the time goes:
time: 135 us; the launch traced here: 134 us
  blocking collectives  71.3 us (53%)
  matrix products  26.2 us (19%)
  local copies, waits for them, and re-layouts  18.1 us (13%)
  waiting for transfers between devices  7.45 us (6%)
  other arithmetic  5.8 us (4%)
  starting transfers between devices  3.93 us (3%)
    all_gather x1, blocking collectives, shards(): lax.all_gather(queries, 'blk', axis=0, tiled=True)  71.3 us
    dot_general x16, matrix products, one_block(): lax.dot_general(flat, piece, (((1,), (1,)), ((), ())), preferred_element_...  26.2 us
    gather x2, local copies, waits for them, and re-layouts, shards(): jnp.take_along_axis(whole, jnp.take(slot_of, candidates, axis=0), axis=1)  9.13 us
    all_to_all x1, waiting for transfers between devices, shards(): lax.all_to_all(table, 'blk', split_axis=0, concat_axis=1, tiled=True)  7.45 us
    gather x2, local copies, waits for them, and re-layouts, shards(): jnp.take(slot_of, candidates, axis=0)  4.54 us
    all_to_all x1, starting transfers between devices, shards(): lax.all_to_all(table, 'blk', split_axis=0, concat_axis=1, tiled=True)  3.93 us
  transfers between devices with their start and end apart: 1, of which 1 were waited for; matrix products, arithmetic and copies ran while one was open for 3% of the time, Pallas kernels for 0%

commit v1 on v0

--- a/solution.py
+++ b/solution.py
@@ -32,7 +32,13 @@
 
 
 def shards(queries, passages, lengths, slot_of, candidates):
-    table = score_table(lax.all_gather(queries, "blk", axis=0, tiled=True), passages, lengths)
+    table = score_table(
+        jnp.concatenate(
+            lax.all_to_all(jnp.stack([queries] * lax.axis_size("blk")), "blk", 0, 0), axis=0
+        ),
+        passages,
+        lengths,
+    )
     whole = lax.all_to_all(table, "blk", split_axis=0, concat_axis=1, tiled=True)
     score = jnp.take_along_axis(whole, jnp.take(slot_of, candidates, axis=0), axis=1)
     top = lax.top_k(score, TOPN)[0]

time: 135 us -> 140 us (1.037)
  the two profiles are of different devices: /device:TPU:86 before, /device:TPU:70 now
where the time goes in v1:
time: 140 us; the launch traced here: 139 us
  starting transfers between devices  50.3 us (36%)
  waiting for transfers between devices  35.8 us (26%)
  matrix products  26.2 us (19%)
  local copies, waits for them, and re-layouts  19.1 us (14%)
  other arithmetic  6.5 us (5%)
    all_to_all x1, starting transfers between devices, shards(): lax.all_to_all(jnp.stack([queries] * lax.axis_size('blk')), 'blk', 0, 0)  43.7 us
    dot_general x16, matrix products, one_block(): lax.dot_general(flat, piece, (((1,), (1,)), ((), ())), preferred_element_...  26.2 us
    all_to_all x1, waiting for transfers between devices, shards(): lax.all_to_all(jnp.stack([queries] * lax.axis_size('blk')), 'blk', 0, 0)  23.5 us
    all_to_all x1, waiting for transfers between devices, shards(): lax.all_to_all(table, 'blk', split_axis=0, concat_axis=1, tiled=True)  12.3 us
    gather x2, local copies, waits for them, and re-layouts, shards(): jnp.take_along_axis(whole, jnp.take(slot_of, candidates, axis=0), axis=1)  9.13 us
    all_to_all x1, starting transfers between devices, shards(): lax.all_to_all(table, 'blk', split_axis=0, concat_axis=1, tiled=True)  6.58 us
    gather x2, local copies, waits for them, and re-layouts, shards(): jnp.take(slot_of, candidates, axis=0)  4.54 us
  transfers between devices with their start and end apart: 2, of which 2 were waited for; matrix products, arithmetic and copies ran while one was open for 4% of the time, Pallas kernels for 0%

profile of v1, /device:TPU:70, one launch (start us, length us, event | category | flops | bytes accessed | tf_op | source)
XLA Modules:
  0.0 139.2 jit_solution(6780456601556637360)
XLA Ops:
  0.6 1.7 %stack.2 = bf16[16,4,32,128]{3,2,1,0:T(8,128)(2,1)} broadcast(bf16[4,32,128]{2,1,0:T(8,128)(2,1)} %param.7), dimensions={1,2,3} | broadcast | bytes 557056 | tf_op jit(solution)/shard_map/stack | solution.py:37
  2.3 43.7 %all-to-all-start = ((bf16[16,4,32,128]{3,2,1,0:T(8,128)(2,1)}), bf16[16,4,32,128]{3,2,1,0:T(8,128)(2,1)S(1)}, u32[]{:S(2)}, u32[]{:S(2)}) async-start(bf16[16,4,32,128]{3,2,1,0:T(8,128)(2,1)} %stack.2), calls=%async_computation | async-start | bytes 1048576 | tf_op jit(solution)/shard_map/all_to_all | solution.py:37
  46.7 4.5 %gather_fusion = s32[1024]{0:T(1024)S(1)} fusion(s32[1024]{0:T(1024)S(1)} %copy-done, s32[1024]{0:T(1024)S(1)} %broadcast_clamp_fusion), kind=kCustom, calls=%fused_computation | custom fusion | bytes 12288 | tf_op jit(solution)/shard_map/jit(_take)/gather | solution.py:43
  51.4 23.5 %all-to-all-done = bf16[16,4,32,128]{3,2,1,0:T(8,128)(2,1)S(1)} async-done(((bf16[16,4,32,128]{3,2,1,0:T(8,128)(2,1)}), bf16[16,4,32,128]{3,2,1,0:T(8,128)(2,1)S(1)}, u32[]{:S(2)}, u32[]{:S(2)}) %all-to-all-start) | async-done | bytes 524320 | tf_op jit(solution)/shard_map/all_to_all | solution.py:37
  74.9 31.6 %while.10 = (s32[]{:T(128)}, f32[16,64,4]{1,2,0:T(4,128)S(1)}, s32[16,4]{1,0:T(8,128)S(1)}, bf16[16,512,128]{2,1,0:T(8,128)(2,1)}, bf16[2048,128]{1,0:T(8,128)(2,1)S(1)}, /*index=5*/s32[]{:T(128)}, f32[]{:T(128)}) while((s32[]{:T(128)}, f32[16,64,4]{1,2,0:T(4,128)S(1)}, s32[16,4]{1,0:T(8,128)S(1)}, bf16[16,512,128]{2,1,0:T(8,128)(2,1)}, ...), condition=%wide.region_3.4_spmd, body=%wide.region_0.3_spmd.sunk | while | flops 270533120 | bytes 793225 | solution.py:30
  75.0 1.6 %select_reduce_fusion.2 = f32[2048,4]{0,1:T(4,128)S(1)} fusion(pred[4,128]{1,0:T(4,128)(4,1)S(1)} %iota_compare_fusion.2, bf16[2048,128]{1,0:T(8,128)(2,1)S(1)} %get-tuple-element.93, bf16[16,512,128]{2,1,0:T(8,128)(2,1)} %get-tuple-element.92, s32[]{:T(128)} %get-tuple-element.82), kind=kOutput, calls=%fused_computation.2.clone.1 | convolution fusion | flops 270524416 | bytes 689152 | tf_op jit(solution)/shard_map/while/body/eval_jaxpr/dot_general | solution.py:22
  77.0 1.6 %select_reduce_fusion.2 = f32[2048,4]{0,1:T(4,128)S(1)} fusion(pred[4,128]{1,0:T(4,128)(4,1)S(1)} %iota_compare_fusion.2, bf16[2048,128]{1,0:T(8,128)(2,1)S(1)} %get-tuple-element.93, bf16[16,512,128]{2,1,0:T(8,128)(2,1)} %get-tuple-element.92, s32[]{:T(128)} %get-tuple-element.82), kind=kOutput, calls=%fused_computation.2.clone.1 | convolution fusion | flops 270524416 | bytes 689152 | tf_op jit(solution)/shard_map/while/body/eval_jaxpr/dot_general | solution.py:22
  78.9 1.6 %select_reduce_fusion.2 = f32[2048,4]{0,1:T(4,128)S(1)} fusion(pred[4,128]{1,0:T(4,128)(4,1)S(1)} %iota_compare_fusion.2, bf16[2048,128]{1,0:T(8,128)(2,1)S(1)} %get-tuple-element.93, bf16[16,512,128]{2,1,0:T(8,128)(2,1)} %get-tuple-element.92, s32[]{:T(128)} %get-tuple-element.82), kind=kOutput, calls=%fused_computation.2.clone.1 | convolution fusion | flops 270524416 | bytes 689152 | tf_op jit(solution)/shard_map/while/body/eval_jaxpr/dot_general | solution.py:22
  80.9 1.6 %select_reduce_fusion.2 = f32[2048,4]{0,1:T(4,128)S(1)} fusion(pred[4,128]{1,0:T(4,128)(4,1)S(1)} %iota_compare_fusion.2, bf16[2048,128]{1,0:T(8,128)(2,1)S(1)} %get-tuple-element.93, bf16[16,512,128]{2,1,0:T(8,128)(2,1)} %get-tuple-element.92, s32[]{:T(128)} %get-tuple-element.82), kind=kOutput, calls=%fused_computation.2.clone.1 | convolution fusion | flops 270524416 | bytes 689152 | tf_op jit(solution)/shard_map/while/body/eval_jaxpr/dot_general | solution.py:22
  82.9 1.6 %select_reduce_fusion.2 = f32[2048,4]{0,1:T(4,128)S(1)} fusion(pred[4,128]{1,0:T(4,128)(4,1)S(1)} %iota_compare_fusion.2, bf16[2048,128]{1,0:T(8,128)(2,1)S(1)} %get-tuple-element.93, bf16[16,512,128]{2,1,0:T(8,128)(2,1)} %get-tuple-element.92, s32[]{:T(128)} %get-tuple-element.82), kind=kOutput, calls=%fused_computation.2.clone.1 | convolution fusion | flops 270524416 | bytes 689152 | tf_op jit(solution)/shard_map/while/body/eval_jaxpr/dot_general | solution.py:22
  84.9 1.6 %select_reduce_fusion.2 = f32[2048,4]{0,1:T(4,128)S(1)} fusion(pred[4,128]{1,0:T(4,128)(4,1)S(1)} %iota_compare_fusion.2, bf16[2048,128]{1,0:T(8,128)(2,1)S(1)} %get-tuple-element.93, bf16[16,512,128]{2,1,0:T(8,128)(2,1)} %get-tuple-element.92, s32[]{:T(128)} %get-tuple-element.82), kind=kOutput, calls=%fused_computation.2.clone.1 | convolution fusion | flops 270524416 | bytes 689152 | tf_op jit(solution)/shard_map/while/body/eval_jaxpr/dot_general | solution.py:22
  86.8 1.6 %select_reduce_fusion.2 = f32[2048,4]{0,1:T(4,128)S(1)} fusion(pred[4,128]{1,0:T(4,128)(4,1)S(1)} %iota_compare_fusion.2, bf16[2048,128]{1,0:T(8,128)(2,1)S(1)} %get-tuple-element.93, bf16[16,512,128]{2,1,0:T(8,128)(2,1)} %get-tuple-element.92, s32[]{:T(128)} %get-tuple-element.82), kind=kOutput, calls=%fused_computation.2.clone.1 | convolution fusion | flops 270524416 | bytes 689152 | tf_op jit(solution)/shard_map/while/body/eval_jaxpr/dot_general | solution.py:22
  88.8 1.6 %select_reduce_fusion.2 = f32[2048,4]{0,1:T(4,128)S(1)} fusion(pred[4,128]{1,0:T(4,128)(4,1)S(1)} %iota_compare_fusion.2, bf16[2048,128]{1,0:T(8,128)(2,1)S(1)} %get-tuple-element.93, bf16[16,512,128]{2,1,0:T(8,128)(2,1)} %get-tuple-element.92, s32[]{:T(128)} %get-tuple-element.82), kind=kOutput, calls=%fused_computation.2.clone.1 | convolution fusion | flops 270524416 | bytes 689152 | tf_op jit(solution)/shard_map/while/body/eval_jaxpr/dot_general | solution.py:22
  92.8 1.6 %select_reduce_fusion.2 = f32[2048,4]{0,1:T(4,128)S(1)} fusion(pred[4,128]{1,0:T(4,128)(4,1)S(1)} %iota_compare_fusion.2, bf16[2048,128]{1,0:T(8,128)(2,1)S(1)} %get-tuple-element.93, bf16[16,512,128]{2,1,0:T(8,128)(2,1)} %get-tuple-element.92, s32[]{:T(128)} %get-tuple-element.82), kind=kOutput, calls=%fused_computation.2.clone.1 | convolution fusion | flops 270524416 | bytes 689152 | tf_op jit(solution)/shard_map/while/body/eval_jaxpr/dot_general | solution.py:22
  94.8 1.6 %select_reduce_fusion.2 = f32[2048,4]{0,1:T(4,128)S(1)} fusion(pred[4,128]{1,0:T(4,128)(4,1)S(1)} %iota_compare_fusion.2, bf16[2048,128]{1,0:T(8,128)(2,1)S(1)} %get-tuple-element.93, bf16[16,512,128]{2,1,0:T(8,128)(2,1)} %get-tuple-element.92, s32[]{:T(128)} %get-tuple-element.82), kind=kOutput, calls=%fused_computation.2.clone.1 | convolution fusion | flops 270524416 | bytes 689152 | tf_op jit(solution)/shard_map/while/body/eval_jaxpr/dot_general | solution.py:22
  96.7 1.6 %select_reduce_fusion.2 = f32[2048,4]{0,1:T(4,128)S(1)} fusion(pred[4,128]{1,0:T(4,128)(4,1)S(1)} %iota_compare_fusion.2, bf16[2048,128]{1,0:T(8,128)(2,1)S(1)} %get-tuple-element.93, bf16[16,512,128]{2,1,0:T(8,128)(2,1)} %get-tuple-element.92, s32[]{:T(128)} %get-tuple-element.82), kind=kOutput, calls=%fused_computation.2.clone.1 | convolution fusion | flops 270524416 | bytes 689152 | tf_op jit(solution)/shard_map/while/body/eval_jaxpr/dot_general | solution.py:22
  98.7 1.6 %select_reduce_fusion.2 = f32[2048,4]{0,1:T(4,128)S(1)} fusion(pred[4,128]{1,0:T(4,128)(4,1)S(1)} %iota_compare_fusion.2, bf16[2048,128]{1,0:T(8,128)(2,1)S(1)} %get-tuple-element.93, bf16[16,512,128]{2,1,0:T(8,128)(2,1)} %get-tuple-element.92, s32[]{:T(128)} %get-tuple-element.82), kind=kOutput, calls=%fused_computation.2.clone.1 | convolution fusion | flops 270524416 | bytes 689152 | tf_op jit(solution)/shard_map/while/body/eval_jaxpr/dot_general | solution.py:22
  100.7 1.6 %select_reduce_fusion.2 = f32[2048,4]{0,1:T(4,128)S(1)} fusion(pred[4,128]{1,0:T(4,128)(4,1)S(1)} %iota_compare_fusion.2, bf16[2048,128]{1,0:T(8,128)(2,1)S(1)} %get-tuple-element.93, bf16[16,512,128]{2,1,0:T(8,128)(2,1)} %get-tuple-element.92, s32[]{:T(128)} %get-tuple-element.82), kind=kOutput, calls=%fused_computation.2.clone.1 | convolution fusion | flops 270524416 | bytes 689152 | tf_op jit(solution)/shard_map/while/body/eval_jaxpr/dot_general | solution.py:22
  102.7 1.6 %select_reduce_fusion.2 = f32[2048,4]{0,1:T(4,128)S(1)} fusion(pred[4,128]{1,0:T(4,128)(4,1)S(1)} %iota_compare_fusion.2, bf16[2048,128]{1,0:T(8,128)(2,1)S(1)} %get-tuple-element.93, bf16[16,512,128]{2,1,0:T(8,128)(2,1)} %get-tuple-element.92, s32[]{:T(128)} %get-tuple-element.82), kind=kOutput, calls=%fused_computation.2.clone.1 | convolution fusion | flops 270524416 | bytes 689152 | tf_op jit(solution)/shard_map/while/body/eval_jaxpr/dot_general | solution.py:22
  104.7 1.6 %select_reduce_fusion.2 = f32[2048,4]{0,1:T(4,128)S(1)} fusion(pred[4,128]{1,0:T(4,128)(4,1)S(1)} %iota_compare_fusion.2, bf16[2048,128]{1,0:T(8,128)(2,1)S(1)} %get-tuple-element.93, bf16[16,512,128]{2,1,0:T(8,128)(2,1)} %get-tuple-element.92, s32[]{:T(128)} %get-tuple-element.82), kind=kOutput, calls=%fused_computation.2.clone.1 | convolution fusion | flops 270524416 | bytes 689152 | tf_op jit(solution)/shard_map/while/body/eval_jaxpr/dot_general | solution.py:22
  107.8 6.6 %all-to-all-start.1 = ((f32[16,1,256]{2,1,0:T(1,128)}), f32[16,1,256]{2,1,0:T(1,128)S(1)}, u32[]{:S(2)}, u32[]{:S(2)}) async-start(f32[16,1,256]{2,1,0:T(1,128)} %reshape.90), calls=%async_computation.1 | async-start | bytes 32768 | tf_op jit(solution)/shard_map/all_to_all | solution.py:42
  114.5 12.3 %all-to-all-done.1 = f32[16,1,256]{2,1,0:T(1,128)S(1)} async-done(((f32[16,1,256]{2,1,0:T(1,128)}), f32[16,1,256]{2,1,0:T(1,128)S(1)}, u32[]{:S(2)}, u32[]{:S(2)}) %all-to-all-start.1) | async-done | bytes 16416 | tf_op jit(solution)/shard_map/all_to_all | solution.py:42
  128.1 9.1 %gather_fusion.1 = f32[1024]{0:T(1024)S(1)} fusion(f32[4,1024]{1,0:T(4,128)S(1)} %all_to_all.21, s32[1024]{0:T(1024)S(1)} %bitcast.43), kind=kCustom, calls=%fused_computation.1 | custom fusion | bytes 16384 | tf_op jit(solution)/shard_map/jit(take_along_axis)/gather | solution.py:43
  137.3 1.9 %sort_prefixfusion = f32[4,10]{1,0:T(4,128)} fusion(f32[4,256]{1,0:T(4,128)S(1)} %and_select_fusion), kind=kCustom, calls=%top_k.9.sort_prefix | custom fusion | flops 10240 | bytes 4256 | tf_op jit(solution)/shard_map/top_k | solution.py:44
  (107 shorter events, 10.0 us)
Async XLA Ops:
  0.6 46.1 %copy-start = (s32[1024]{0:T(1024)S(1)}, s32[1024]{0:T(1024)}, u32[]{:S(2)}) copy-start(s32[1024]{0:T(1024)} %param.10) | copy-start | bytes 12292
  2.3 72.6 %all-to-all-start = ((bf16[16,4,32,128]{3,2,1,0:T(8,128)(2,1)}), bf16[16,4,32,128]{3,2,1,0:T(8,128)(2,1)S(1)}, u32[]{:S(2)}, u32[]{:S(2)}) async-start(bf16[16,4,32,128]{3,2,1,0:T(8,128)(2,1)} %stack.2), calls=%async_computation | async-start | bytes 1048576 | tf_op jit(solution)/shard_map/all_to_all | solution.py:37
  46.7 4.6 %copy-start.3 = (s32[64]{0:T(128)S(1)}, s32[64]{0:T(128)}, u32[]{:S(2)}) copy-start(s32[64]{0:T(128)} %param.9) | copy-start | bytes 772
  74.9 39.5 %copy-start.1 = (s32[4,256]{1,0:T(4,128)S(1)}, s32[4,256]{1,0:T(4,128)}, u32[]{:S(2)}) copy-start(s32[4,256]{1,0:T(4,128)} %param.11) | copy-start | bytes 12292
  107.8 18.9 %all-to-all-start.1 = ((f32[16,1,256]{2,1,0:T(1,128)}), f32[16,1,256]{2,1,0:T(1,128)S(1)}, u32[]{:S(2)}, u32[]{:S(2)}) async-start(f32[16,1,256]{2,1,0:T(1,128)} %reshape.90), calls=%async_computation.1 | async-start | bytes 32768 | tf_op jit(solution)/shard_map/all_to_all | solution.py:42
  137.3 1.9 %copy-start.2 = (f32[4,256]{1,0:T(4,128)}, f32[4,256]{1,0:T(4,128)S(1)}, u32[]{:S(2)}) copy-start(f32[4,256]{1,0:T(4,128)S(1)} %and_select_fusion) | copy-start | bytes 12292
